TPU v7x, 32 devices: a whole 2x2x4 slice. The times are simulated.
32 devices in a mesh: expert: 4 (over z), tensor: 8 (over y, x, core).
Axes of the slice: x: 2, y: 2, z: 4, core: 2. Of those that a mesh axis runs over, the one named last changes fastest.
Arguments:
- expert_inputs: bfloat16 [8, 64, 4096], P('expert'), may hold values from -6 to 6
- gates: float32 [8, 64], P('expert'), may hold values from 0.2 to 1
- chosen_tokens: int32 [8, 64], replicated, may hold values from 0 to 4095, as said below
- w_gate: bfloat16 [8, 4096, 1792], P('expert', None, 'tensor'), may hold values from -0.09375 to 0.09375
- w_up: bfloat16 [8, 4096, 1792], P('expert', None, 'tensor'), may hold values from -0.09375 to 0.09375
- w_down: bfloat16 [8, 1792, 4096], P('expert', 'tensor'), may hold values from -0.125 to 0.125
- residual: bfloat16 [4096, 4096], P(('expert', 'tensor')), may hold values from -6 to 6
- norm_gain: float32 [4096], replicated, may hold values from 0.5 to 1.5
- w_qkv: bfloat16 [4096, 12288], P(None, 'tensor'), may hold values from -0.09375 to 0.09375
Outputs:
- stream: bfloat16 [4096, 4096], P(('expert', 'tensor'))
- projected: bfloat16 [4096, 12288], P('expert', 'tensor')
Inputs may be any that keep to these rules, and one draw needn't show every extreme that they name: `chosen_tokens`: each row holds 64 different token indices; at most 4 of a row lie in one block of 128 consecutive tokens, and in every draw some block holds 4 tokens of every row.
All inputs are finite; a program needn't handle non-finite values.
Results may differ from a plain program's by a relative error of at most 0.005.
Values may be sent and summed in bfloat16 or wider, within the bound.
A program may use at most 128 MiB of HBM per device.

v0:
```python
import functools

import jax
import jax.numpy as jnp
from jax import lax
from jax.experimental import pallas as pl
from jax.experimental.pallas import tpu as pltpu
from jax.sharding import PartitionSpec as P

MOST = 4
MESH = pl.DeviceIdType.MESH


def finish_kernel(
    row_steps,
    order,
    owner_ref,
    slots_ref,
    residual_ref,
    rows_ref,
    gain_ref,
    weight_ref,
    stream_ref,
    projected_ref,
    combined_ref,
    normed_ref,
):
    step = pl.program_id(0)
    tok_rows, feature_width = residual_ref.shape
    chunk = rows_ref.shape[2]

    @pl.when(step < row_steps)
    def _():
        tokens = lax.broadcasted_iota(jnp.int32, (tok_rows, slots_ref.shape[1]), 0)
        placement = jnp.where(slots_ref[...] == tokens + step * tok_rows, 1.0, 0.0).astype(
            jnp.bfloat16
        )
        squares = jnp.zeros((tok_rows, 128), jnp.float32)
        for place, start in enumerate(range(0, feature_width, chunk)):
            cols = pl.ds(start, chunk)
            combined = residual_ref[:, cols].astype(jnp.float32) + jnp.dot(
                placement, rows_ref[order[place]], preferred_element_type=jnp.float32
            )
            combined_ref[:, cols] = combined
            for part in range(0, chunk, 128):
                piece = combined[:, part : part + 128]
                squares = squares + piece * piece
        mean = jnp.sum(squares, axis=1, keepdims=True) / feature_width
        scale = lax.rsqrt(mean + 1e-06)
        begin = pl.multiple_of(step * tok_rows, tok_rows)
        for start in range(0, feature_width, chunk):
            cols = pl.ds(start, chunk)
            normed_ref[pl.ds(begin, tok_rows), cols] = (
                combined_ref[:, cols] * scale * gain_ref[:, cols]
            ).astype(jnp.bfloat16)

        @pl.when(step == owner_ref[0])
        def _():
            stream_ref[...] = combined_ref[...].astype(jnp.bfloat16)

    @pl.when(step >= row_steps)
    def _():
        projected_ref[...] = jnp.dot(
            normed_ref[...], weight_ref[...], preferred_element_type=jnp.float32
        ).astype(jnp.bfloat16)


def finish(owner, slots, residual_all, rows, order, gain, w_qkv, tok_rows):
    total_rows, feature_width = residual_all.shape
    columns = w_qkv.shape[1]
    tile = 256
    row_steps = total_rows // tok_rows
    col_steps = columns // tile
    slot_total = rows.shape[1]
    return pl.pallas_call(
        functools.partial(finish_kernel, row_steps, order),
        grid=(row_steps + col_steps,),
        in_specs=[
            pl.BlockSpec(memory_space=pltpu.SMEM),
            pl.BlockSpec((1, slot_total), lambda i: (0, 0)),
            pl.BlockSpec((tok_rows, feature_width), lambda i: (jnp.minimum(i, row_steps - 1), 0)),
            pl.BlockSpec(rows.shape, lambda i: (0, 0, 0)),
            pl.BlockSpec((1, feature_width), lambda i: (0, 0)),
            pl.BlockSpec((feature_width, tile), lambda i: (0, jnp.maximum(i - row_steps, 0))),
        ],
        out_specs=[
            pl.BlockSpec((tok_rows, feature_width), lambda i: (0, 0)),
            pl.BlockSpec((total_rows, tile), lambda i: (0, jnp.maximum(i - row_steps, 0))),
        ],
        out_shape=[
            jax.ShapeDtypeStruct((tok_rows, feature_width), jnp.bfloat16),
            jax.ShapeDtypeStruct((total_rows, columns), jnp.bfloat16),
        ],
        scratch_shapes=[
            pltpu.VMEM((tok_rows, feature_width), jnp.float32),
            pltpu.VMEM((total_rows, feature_width), jnp.bfloat16),
        ],
        compiler_params=pltpu.CompilerParams(
            vmem_limit_bytes=60 * 1024 * 1024, dimension_semantics=("arbitrary",)
        ),
        cost_estimate=pl.CostEstimate(
            flops=2 * total_rows * feature_width * (columns + slot_total),
            bytes_accessed=2 * (feature_width * columns + total_rows * columns),
            transcendentals=0,
        ),
    )(owner, slots, residual_all, rows, gain, w_qkv)


def comm_kernel(
    groups,
    inputs_ref,
    gates_ref,
    table_ref,
    gate_hbm,
    up_hbm,
    down_hbm,
    residual_hbm,
    slots_ref,
    gain_ref,
    weight_hbm,
    stream_ref,
    projected_hbm,
    gate_w,
    up_w,
    down_w,
    weight,
    blocks,
    rows,
    combined_ref,
    normed_ref,
    staged,
    partial,
    half_in,
    chips_sum,
    chips_in,
    outgoing,
    load_sem,
    first_send,
    first_recv,
    reduce_send,
    reduce_recv,
    group_send,
    group_recv,
    block_send,
    block_recv,
    row_send,
    row_recv,
    store_sem,
):
    group = lax.axis_index("expert")
    me = lax.axis_index("tensor")
    core = me % 2
    partner = me + 1 - 2 * core
    along_x = me + 2 - 4 * ((me // 2) % 2)
    along_y = me + 4 - 8 * (me // 4)
    across = along_x + 4 - 8 * (me // 4)
    local_experts, slot_count, feature_width = inputs_ref.shape
    chips, row_total, width = chips_sum.shape

    def send(source, target, send_sem, recv_sem, device):
        copy = pltpu.make_async_remote_copy(
            src_ref=source,
            dst_ref=target,
            send_sem=send_sem,
            recv_sem=recv_sem,
            device_id=device,
            device_id_type=MESH,
        )
        copy.start()
        return copy

    tok_rows = residual_hbm.shape[0]
    loads = [pltpu.make_async_copy(residual_hbm, blocks.at[me], load_sem.at[0])]
    for index, (hbm, vmem) in enumerate(((gate_hbm, gate_w), (up_hbm, up_w), (down_hbm, down_w))):
        loads.append(pltpu.make_async_copy(hbm, vmem, load_sem.at[index + 1]))
    for copy in loads:
        copy.start()
    load_weight = pltpu.make_async_copy(weight_hbm, weight, load_sem.at[4])
    load_weight.start()

    barrier = pltpu.get_barrier_semaphore()
    peers = [(group, device) for device in (partner, along_x, along_y, across)]
    peers += [((group + d) % groups, me) for d in range(1, groups)]
    for device in peers:
        pl.semaphore_signal(barrier, inc=1, device_id=device, device_id_type=MESH)
    pl.semaphore_wait(barrier, len(peers))

    half, quarter, groups_half = tok_rows // 2, tok_rows // 4, groups // 2
    corner = (me, along_x, along_y, across)

    def block_send_to(index, origin, start, size, device):
        part = blocks.at[origin, pl.ds(start, size)]
        return send(part, part, block_send.at[index], block_recv.at[index], (group, device))

    def row_send_to(index, origin, start, size, device):
        part = rows.at[origin, pl.ds(start, size)]
        return send(part, part, row_send.at[index], row_recv.at[index], (group, device))

    def block_partner(role):
        return block_send_to(8 + role, corner[role], 0, tok_rows, partner)

    def row_partner(role):
        return row_send_to(6 + role, corner[role], 0, groups, partner)

    loads[0].wait()
    block_x0 = block_send_to(0, me, 0, half, along_x)
    block_y0 = block_send_to(1, me, half, half, along_y)
    block_own = block_partner(0)

    for copy in loads[1:]:
        copy.wait()
    contract = (((1,), (1,)), ((), ()))
    for expert in range(local_experts):
        gate_part = lax.dot_general(
            inputs_ref[expert], gate_w[expert], contract, preferred_element_type=jnp.float32
        )
        up_part = lax.dot_general(
            inputs_ref[expert], up_w[expert], contract, preferred_element_type=jnp.float32
        )
        hidden = (gate_part / (1.0 + jnp.exp(-gate_part)) * up_part).astype(jnp.bfloat16)
        lines = pl.ds(expert * slot_count, slot_count)
        for place in range(2 * chips):
            value = jnp.dot(
                hidden,
                down_w[expert, :, place * width : (place + 1) * width],
                preferred_element_type=jnp.float32,
            )
            partial[place, lines, :] = (value * gates_ref[expert]).astype(jnp.bfloat16)

    first = send(
        partial.at[pl.ds((1 - core) * chips, chips)],
        half_in,
        first_send,
        first_recv,
        (group, partner),
    )
    first.wait_recv()
    for chip in range(chips):
        chips_sum[chip] = (
            partial[core * chips + chip].astype(jnp.float32) + half_in[chip].astype(jnp.float32)
        ).astype(jnp.bfloat16)
    reduces = [
        send(
            chips_sum.at[device // 2],
            chips_in.at[index],
            reduce_send.at[index],
            reduce_recv.at[index],
            (group, device),
        )
        for index, device in enumerate((across, along_x, along_y))
    ]
    block_x1 = block_send_to(2, me, half, quarter, along_x)
    block_y1 = block_send_to(3, me, 0, quarter, along_y)
    for copy in reduces:
        copy.wait_recv()
    total = chips_sum[me // 2].astype(jnp.float32)
    for index in range(3):
        total = total + chips_in[index].astype(jnp.float32)
    total = total.astype(jnp.bfloat16)
    for place in range(groups):
        outgoing[place] = jnp.dot(
            table_ref[place], total, preferred_element_type=jnp.float32
        ).astype(jnp.bfloat16)
    exchanges = [
        send(
            outgoing.at[(group + d) % groups],
            rows.at[me, group],
            group_send.at[d - 1],
            group_recv.at[d - 1],
            ((group + d) % groups, me),
        )
        for d in range(1, groups)
    ]
    rows[me, group] = outgoing[group]
    for copy in exchanges:
        copy.wait_recv()
    rest = groups - groups_half
    row_x0 = row_send_to(0, me, 0, groups_half, along_x)
    row_y0 = row_send_to(1, me, groups_half, rest, along_y)
    row_x1 = row_send_to(2, me, groups_half, rest, along_x)
    row_y1 = row_send_to(3, me, 0, groups_half, along_y)
    row_own = row_partner(0)
    row_x0.wait_recv()
    row_ox = row_send_to(4, along_x, 0, groups_half, along_y)
    row_y0.wait_recv()
    row_oy = row_send_to(5, along_y, groups_half, rest, along_x)
    block_x2 = block_send_to(4, me, half + quarter, quarter, along_x)
    block_y2 = block_send_to(5, me, quarter, quarter, along_y)
    block_x0.wait_recv()
    block_ox = block_send_to(6, along_x, 0, half, along_y)
    block_y0.wait_recv()
    block_oy = block_send_to(7, along_y, half, half, along_x)
    row_x1.wait_recv()
    row_px = row_partner(1)
    row_y1.wait_recv()
    row_py = row_partner(2)
    row_ox.wait_recv()
    row_oy.wait_recv()
    row_pd = row_partner(3)
    block_own.wait_recv()
    for copy in (row_own, row_px, row_py, row_pd):
        copy.wait_recv()
    load_weight.wait()

    pair = 2 * tok_rows
    slot_total = slots_ref.shape[1]
    tile = 512
    col_tiles = weight.shape[1] // tile
    stores = []

    def finish_pair(step, chip):
        tokens = lax.broadcasted_iota(jnp.int32, (pair, slot_total), 0) + chip * pair
        placement = jnp.where(slots_ref[...] == tokens, 1.0, 0.0).astype(jnp.bfloat16)

        def place(index, squares):
            cols = pl.ds(pl.multiple_of(index * width, width), width)
            source = (index % chips) * 2 + index // chips
            values = rows[source].reshape(slot_total, width)
            block = blocks[pl.ds(2 * chip, 2), :, cols].reshape(pair, width)
            combined = block.astype(jnp.float32) + jnp.dot(
                placement, values, preferred_element_type=jnp.float32
            )
            combined_ref[:, cols] = combined
            for part in range(0, width, 128):
                piece = combined[:, part : part + 128]
                squares = squares + piece * piece
            return squares

        squares = lax.fori_loop(0, 2 * chips, place, jnp.zeros((pair, 128), jnp.float32), unroll=2)
        scale = lax.rsqrt(jnp.sum(squares, axis=1, keepdims=True) / feature_width + 1e-06)

        def norm(index, carry):
            cols = pl.ds(pl.multiple_of(index * width, width), width)
            normed_ref[:, cols] = (combined_ref[:, cols] * scale * gain_ref[:, cols]).astype(
                jnp.bfloat16
            )
            return carry

        lax.fori_loop(0, 2 * chips, norm, 0, unroll=2)
        if step == 0:
            begin = pl.multiple_of(core * tok_rows, tok_rows)
            stream_ref[...] = combined_ref[pl.ds(begin, tok_rows), :].astype(jnp.bfloat16)

        def project(index, carry):
            cols = pl.ds(pl.multiple_of(index * tile, tile), tile)
            staged[step, :, cols] = jnp.dot(
                normed_ref[...], weight[:, cols], preferred_element_type=jnp.float32
            ).astype(jnp.bfloat16)
            return carry

        lax.fori_loop(0, col_tiles, project, 0)
        begin = pl.multiple_of(chip * pair, pair)
        store = pltpu.make_async_copy(
            staged.at[step], projected_hbm.at[pl.ds(begin, pair)], store_sem.at[step]
        )
        store.start()
        stores.append(store)

    finish_pair(0, me // 2)
    block_x1.wait_recv()
    block_x2.wait_recv()
    block_px = block_partner(1)
    block_y1.wait_recv()
    block_y2.wait_recv()
    block_py = block_partner(2)
    block_px.wait_recv()
    finish_pair(1, along_x // 2)
    block_ox.wait_recv()
    block_oy.wait_recv()
    block_pd = block_partner(3)
    block_py.wait_recv()
    finish_pair(2, along_y // 2)
    block_pd.wait_recv()
    finish_pair(3, across // 2)

    sent = [block_own, block_px, block_py, block_pd, row_own, row_px, row_py, row_pd]
    sent += reduces + exchanges + [first, block_x0, block_x1, block_x2]
    sent += [block_y0, block_y1, block_y2, block_ox, block_oy]
    sent += [row_x0, row_x1, row_y0, row_y1, row_ox, row_oy]
    for copy in sent:
        copy.wait_send()
    for store in stores:
        store.wait()


def communicate(
    groups, members, table, inputs, gates, w_gate, w_up, w_down, residual, slots, gain, w_qkv
):
    local_experts, slot_count, feature_width = inputs.shape
    tok_rows = residual.shape[0]
    row_total = local_experts * slot_count
    width = feature_width // members
    chips = members // 2
    keep = table.shape[1]
    bf16 = jnp.bfloat16
    anywhere = pl.BlockSpec(memory_space=pl.ANY)
    vmem = pl.BlockSpec(memory_space=pltpu.VMEM)
    dma = pltpu.SemaphoreType.DMA
    gate_t, up_t = jnp.swapaxes(w_gate, 1, 2), jnp.swapaxes(w_up, 1, 2)
    return pl.pallas_call(
        functools.partial(comm_kernel, groups),
        in_specs=[vmem] * 3 + [anywhere] * 4 + [vmem, vmem, anywhere],
        out_specs=[vmem, anywhere],
        out_shape=[
            jax.ShapeDtypeStruct((tok_rows, feature_width), bf16),
            jax.ShapeDtypeStruct((members * tok_rows, w_qkv.shape[1]), bf16),
        ],
        scratch_shapes=[
            pltpu.VMEM(gate_t.shape, bf16),
            pltpu.VMEM(up_t.shape, bf16),
            pltpu.VMEM(w_down.shape, bf16),
            pltpu.VMEM(w_qkv.shape, bf16),
            pltpu.VMEM((members, tok_rows, feature_width), bf16),
            pltpu.VMEM((members, groups, keep, width), bf16),
            pltpu.VMEM((2 * tok_rows, feature_width), jnp.float32),
            pltpu.VMEM((2 * tok_rows, feature_width), bf16),
            pltpu.VMEM((chips, 2 * tok_rows, w_qkv.shape[1]), bf16),
            pltpu.VMEM((members, row_total, width), bf16),
            pltpu.VMEM((chips, row_total, width), bf16),
            pltpu.VMEM((chips, row_total, width), bf16),
            pltpu.VMEM((chips - 1, row_total, width), bf16),
            pltpu.VMEM((groups, keep, width), bf16),
            dma((5,)),
            dma,
            dma,
            dma((3,)),
            dma((3,)),
            dma((groups - 1,)),
            dma((groups - 1,)),
            dma((12,)),
            dma((12,)),
            dma((10,)),
            dma((10,)),
            dma((chips,)),
        ],
        compiler_params=pltpu.CompilerParams(
            collective_id=0, has_side_effects=True, vmem_limit_bytes=60 * 1024 * 1024
        ),
    )(inputs, gates[:, :, None], table, gate_t, up_t, w_down, residual, slots, gain, w_qkv)


def plain_rows(
    expert_inputs, gates, w_gate, w_up, w_down, send_table, expert_count, tensor_count
):
    local_experts, slot_count, feature_width = expert_inputs.shape
    gate_part = jnp.einsum(
        "ecd,edf->ecf", expert_inputs, w_gate, preferred_element_type=jnp.float32
    )
    up_part = jnp.einsum("ecd,edf->ecf", expert_inputs, w_up, preferred_element_type=jnp.float32)
    hidden = (jax.nn.silu(gate_part) * up_part).astype(jnp.bfloat16)
    partial_value = (
        jnp.einsum("ecf,efd->ecd", hidden, w_down, preferred_element_type=jnp.float32)
        * gates[:, :, None]
    ).astype(jnp.bfloat16)
    row_total = local_experts * slot_count
    arrived = lax.all_to_all(
        partial_value.reshape(row_total, feature_width),
        "tensor",
        split_axis=1,
        concat_axis=0,
        tiled=True,
    ).reshape(tensor_count, local_experts, slot_count, -1)
    summed = jnp.sum(arrived.astype(jnp.float32), axis=0).astype(jnp.bfloat16)

    outgoing = jnp.einsum("zlkmj,mjf->zlkf", send_table, summed)
    incoming = lax.all_to_all(
        outgoing.reshape(expert_count, -1, outgoing.shape[-1]),
        "expert",
        split_axis=0,
        concat_axis=0,
        tiled=True,
    )
    incoming = incoming.reshape(-1, outgoing.shape[-1])
    return lax.all_gather(incoming, "tensor", axis=0, tiled=False)


def per_device(
    expert_inputs, gates, chosen_tokens, w_gate, w_up, w_down, residual, norm_gain, w_qkv
):
    expert_count = lax.axis_size("expert")
    tensor_count = lax.axis_size("tensor")
    my_group = lax.axis_index("expert")
    local_experts, slot_count, feature_width = expert_inputs.shape
    tok_rows = residual.shape[0]
    group_rows = tok_rows * tensor_count
    keep = min(slot_count, MOST * tensor_count)

    dest = chosen_tokens // group_rows
    earlier = jnp.arange(slot_count)[None, :] < jnp.arange(slot_count)[:, None]
    rank = jnp.sum(
        ((dest[:, :, None] == dest[:, None, :]) & earlier[None]).astype(jnp.int32), axis=2
    )
    kept = jnp.arange(keep, dtype=jnp.int32)
    mine = jnp.where(dest == my_group, rank, -1)
    token_at = jnp.sum(
        jnp.where(
            mine[:, None, :] == kept[None, :, None],
            (chosen_tokens % group_rows)[:, None, :] + 1,
            0,
        ),
        axis=2,
    ).reshape(1, -1) - 1

    local_dest = lax.dynamic_slice_in_dim(dest, my_group * local_experts, local_experts, 0)
    local_rank = lax.dynamic_slice_in_dim(rank, my_group * local_experts, local_experts, 0)
    send_table = (
        (local_dest[None, :, None, :] == jnp.arange(expert_count)[:, None, None, None])
        & (local_rank[None, :, None, :] == kept[None, None, :, None])
    ).astype(jnp.bfloat16)
    same = jnp.eye(local_experts, dtype=jnp.bfloat16)
    send_table = send_table[:, :, :, None, :] * same[None, :, None, :, None]
    if tensor_count == 8:
        return communicate(
            expert_count,
            tensor_count,
            send_table.reshape(expert_count, local_experts * keep, -1),
            expert_inputs,
            gates,
            w_gate,
            w_up,
            w_down,
            residual,
            token_at,
            norm_gain[None, :],
            w_qkv,
        )
    residual_all = lax.all_gather(residual, "tensor", axis=0, tiled=True)
    rows = plain_rows(
        expert_inputs, gates, w_gate, w_up, w_down, send_table, expert_count, tensor_count
    )
    order = tuple(range(tensor_count))
    return finish(
        lax.axis_index("tensor").reshape(1),
        token_at,
        residual_all,
        rows,
        order,
        norm_gain[None, :],
        w_qkv,
        tok_rows,
    )


def solution(mesh):
    return jax.shard_map(
        per_device,
        mesh=mesh,
        in_specs=(
            P("expert", None, None),
            P("expert", None),
            P(),
            P("expert", None, "tensor"),
            P("expert", None, "tensor"),
            P("expert", "tensor", None),
            P(("expert", "tensor"), None),
            P(),
            P(None, "tensor"),
        ),
        out_specs=(P(("expert", "tensor"), None), P("expert", "tensor")),
        check_vma=False,
    )
```

profile of v0, /device:TPU:0, one launch (start us, length us, event | category | flops | bytes accessed | tf_op | source)
XLA Modules:
  0.0 81.8 jit_solution(1705309520412523330)
XLA Ops:
  0.6 0.7 add_select_fusion.1
  1.4 0.3 convert_reduce_fusion
  1.7 0.7 compare_select_fusion
  2.4 0.2 select_reduce_fusion
  2.6 0.6 sub.14.slots_ref
  3.3 0.1 mul.27
  3.4 0.1 mul.28
  3.5 0.1 mul.25
  3.6 0.1 mul.26
  3.7 0.6 broadcast_multiply_fusion.table_ref
  4.4 1.4 %copy.12.gates_ref = f32[2,64,1]{2,1,0:T(8,128)} copy(f32[2,64,1]{1,0,2:T(2,128)} %bitcast.7) | data formatting | bytes 1024 | tf_op jit(solution)/shard_map/broadcast_in_dim | solution.py:439
  5.8 70.0 %shard_map.104 = (bf16[128,4096]{1,0:T(8,128)(2,1)}, bf16[1024,1536]{1,0:T(8,128)(2,1)}) custom-call(bf16[2,64,4096]{2,1,0:T(8,128)(2,1)} %inputs_ref.1, f32[2,64,1]{2,1,0:T(8,128)} %copy.12.gates_ref, bf16[4,64,128]{2,1,0:T(8,128)(2,1)} %broadcast_multiply_fusion.table_ref, bf16[2,224,4096]{2,1,0:T(8,128)(2,1)} %bitcast.4, bf16[2,224,4096]{2,1,0:T(8,128)(2,1)} %bitcast.5, ...), custom_call_target="tpu_custom_call" | custom-call | tf_op jit(solution)/shard_map/pallas_call | solution.py:400
  75.8 2.3 %copy.15 = bf16[128,4096]{1,0:T(8,128)(2,1)} copy(bf16[128,4096]{1,0:T(8,128)(2,1)} %get-tuple-element.8) | data formatting | bytes 2097152
  78.1 3.8 %copy.16 = bf16[1024,1536]{1,0:T(8,128)(2,1)} copy(bf16[1024,1536]{1,0:T(8,128)(2,1)} %get-tuple-element.9) | data formatting | bytes 6291456
  (7 shorter events, 0.1 us)
where the time goes:
time: 82.1 us; the launch traced here: 81.8 us
  Pallas kernels  70 us (85%)
  local copies, waits for them, and re-layouts  8.48 us (10%)
  other arithmetic  2.62 us (3%)
    pallas_call x1, Pallas kernels, communicate(): pl.pallas_call(functools.partial(comm_kernel, groups), in_specs=[vmem] *...  70 us
    unnamed x2, local copies, waits for them, and re-layouts  6.04 us

commit v1 on v0

v1 whole, which is shorter than its diff:
```python
import functools

import jax
import jax.numpy as jnp
from jax import lax
from jax.experimental import pallas as pl
from jax.experimental.pallas import tpu as pltpu
from jax.sharding import PartitionSpec as P

MOST = 4
MESH = pl.DeviceIdType.MESH


def finish_kernel(
    row_steps,
    order,
    owner_ref,
    slots_ref,
    residual_ref,
    rows_ref,
    gain_ref,
    weight_ref,
    stream_ref,
    projected_ref,
    combined_ref,
    normed_ref,
):
    step = pl.program_id(0)
    tok_rows, feature_width = residual_ref.shape
    chunk = rows_ref.shape[2]

    @pl.when(step < row_steps)
    def _():
        tokens = lax.broadcasted_iota(jnp.int32, (tok_rows, slots_ref.shape[1]), 0)
        placement = jnp.where(slots_ref[...] == tokens + step * tok_rows, 1.0, 0.0).astype(
            jnp.bfloat16
        )
        squares = jnp.zeros((tok_rows, 128), jnp.float32)
        for place, start in enumerate(range(0, feature_width, chunk)):
            cols = pl.ds(start, chunk)
            combined = residual_ref[:, cols].astype(jnp.float32) + jnp.dot(
                placement, rows_ref[order[place]], preferred_element_type=jnp.float32
            )
            combined_ref[:, cols] = combined
            for part in range(0, chunk, 128):
                piece = combined[:, part : part + 128]
                squares = squares + piece * piece
        mean = jnp.sum(squares, axis=1, keepdims=True) / feature_width
        scale = lax.rsqrt(mean + 1e-06)
        begin = pl.multiple_of(step * tok_rows, tok_rows)
        for start in range(0, feature_width, chunk):
            cols = pl.ds(start, chunk)
            normed_ref[pl.ds(begin, tok_rows), cols] = (
                combined_ref[:, cols] * scale * gain_ref[:, cols]
            ).astype(jnp.bfloat16)

        @pl.when(step == owner_ref[0])
        def _():
            stream_ref[...] = combined_ref[...].astype(jnp.bfloat16)

    @pl.when(step >= row_steps)
    def _():
        projected_ref[...] = jnp.dot(
            normed_ref[...], weight_ref[...], preferred_element_type=jnp.float32
        ).astype(jnp.bfloat16)


def finish(owner, slots, residual_all, rows, order, gain, w_qkv, tok_rows):
    total_rows, feature_width = residual_all.shape
    columns = w_qkv.shape[1]
    tile = 256
    row_steps = total_rows // tok_rows
    col_steps = columns // tile
    slot_total = rows.shape[1]
    return pl.pallas_call(
        functools.partial(finish_kernel, row_steps, order),
        grid=(row_steps + col_steps,),
        in_specs=[
            pl.BlockSpec(memory_space=pltpu.SMEM),
            pl.BlockSpec((1, slot_total), lambda i: (0, 0)),
            pl.BlockSpec((tok_rows, feature_width), lambda i: (jnp.minimum(i, row_steps - 1), 0)),
            pl.BlockSpec(rows.shape, lambda i: (0, 0, 0)),
            pl.BlockSpec((1, feature_width), lambda i: (0, 0)),
            pl.BlockSpec((feature_width, tile), lambda i: (0, jnp.maximum(i - row_steps, 0))),
        ],
        out_specs=[
            pl.BlockSpec((tok_rows, feature_width), lambda i: (0, 0)),
            pl.BlockSpec((total_rows, tile), lambda i: (0, jnp.maximum(i - row_steps, 0))),
        ],
        out_shape=[
            jax.ShapeDtypeStruct((tok_rows, feature_width), jnp.bfloat16),
            jax.ShapeDtypeStruct((total_rows, columns), jnp.bfloat16),
        ],
        scratch_shapes=[
            pltpu.VMEM((tok_rows, feature_width), jnp.float32),
            pltpu.VMEM((total_rows, feature_width), jnp.bfloat16),
        ],
        compiler_params=pltpu.CompilerParams(
            vmem_limit_bytes=60 * 1024 * 1024, dimension_semantics=("arbitrary",)
        ),
        cost_estimate=pl.CostEstimate(
            flops=2 * total_rows * feature_width * (columns + slot_total),
            bytes_accessed=2 * (feature_width * columns + total_rows * columns),
            transcendentals=0,
        ),
    )(owner, slots, residual_all, rows, gain, w_qkv)


def comm_kernel(
    groups,
    keep,
    inputs_hbm,
    gates_hbm,
    tokens_hbm,
    gain_hbm,
    gate_hbm,
    up_hbm,
    down_hbm,
    residual_hbm,
    weight_hbm,
    stream_ref,
    projected_ref,
    inputs,
    gates,
    tokens,
    gain,
    gate_w,
    up_w,
    down_w,
    raw,
    weight,
    blocks,
    rows,
    acc,
    row_acc,
    row_out,
    ranks,
    slot_col,
    slots,
    scales,
    partial,
    half_in,
    chips_sum,
    chips_in,
    outgoing,
    load_sem,
    expert_sem,
    first_send,
    first_recv,
    reduce_send,
    reduce_recv,
    group_send,
    group_recv,
    link_send,
    link_recv,
    pair_send,
    pair_recv,
    row_send,
    row_recv,
    scale_send,
    scale_recv,
):
    group = lax.axis_index("expert")
    me = lax.axis_index("tensor")
    core = me % 2
    partner = me + 1 - 2 * core
    along_x = me + 2 - 4 * ((me // 2) % 2)
    along_y = me + 4 - 8 * (me // 4)
    across = along_x + 4 - 8 * (me // 4)
    local_experts, slot_count, feature_width = inputs.shape
    chips, row_total, width = chips_sum.shape
    members, units, tok_rows, _ = blocks.shape
    pair = 2 * tok_rows
    half_units = units // 2
    group_rows = members * tok_rows
    slot_total = slots.shape[1]
    tile = 512
    col_tiles = weight.shape[1] // tile
    f32, bf16 = jnp.float32, jnp.bfloat16

    def load(source, target, sem):
        copy = pltpu.make_async_copy(source, target, sem)
        copy.start()
        return copy

    load_tokens = load(tokens_hbm, tokens, load_sem.at[0])
    load_gates = load(gates_hbm, gates, load_sem.at[1])
    load_gain = load(gain_hbm, gain, load_sem.at[2])
    load_raw = load(residual_hbm, raw, load_sem.at[3])
    load_inputs = load(inputs_hbm, inputs, load_sem.at[4])
    load_experts = [
        [
            load(hbm.at[expert], vmem.at[expert], expert_sem.at[3 * expert + index])
            for index, (hbm, vmem) in enumerate(
                ((gate_hbm, gate_w), (up_hbm, up_w), (down_hbm, down_w))
            )
        ]
        for expert in range(local_experts)
    ]
    load_weight = load(weight_hbm, weight, load_sem.at[5])

    barrier = pltpu.get_barrier_semaphore()
    peers = [(group, lax.rem(me + d, members)) for d in range(1, members)]
    peers += [((group + d) % groups, me) for d in range(1, groups)]
    for device in peers:
        pl.semaphore_signal(barrier, inc=1, device_id=device, device_id_type=MESH)

    sent = []

    def send(source, target, send_sem, recv_sem, device):
        copy = pltpu.make_async_remote_copy(
            src_ref=source,
            dst_ref=target,
            send_sem=send_sem,
            recv_sem=recv_sem,
            device_id=(group, device),
            device_id_type=MESH,
        )
        copy.start()
        sent.append(copy)
        return copy

    def on_link(index, origin, unit, device):
        part = blocks.at[origin, unit]
        return send(part, part, link_send.at[index], link_recv.at[index], device)

    def own_x(unit):
        return on_link(unit, me, unit, along_x)

    def own_y(unit):
        return on_link(units + unit, me, unit, along_y)

    def relay(unit):
        if unit < half_units:
            return on_link(2 * units + unit, along_x, unit, along_y)
        return on_link(2 * units + unit, along_y, unit, along_x)

    def to_partner(role, unit):
        part = blocks.at[(along_x, along_y, across)[role], unit]
        index = role * units + unit
        return send(part, part, pair_send.at[index], pair_recv.at[index], partner)

    def rows_to(index, origin, start, size, device):
        part = rows.at[origin, pl.ds(start, size)]
        return send(part, part, row_send.at[index], row_recv.at[index], device)

    def eye(size):
        shape = (size, size)
        return lax.broadcasted_iota(jnp.int32, shape, 0) == lax.broadcasted_iota(
            jnp.int32, shape, 1
        )

    def column(row):
        return jnp.sum(jnp.where(eye(row.shape[1]), row, 0.0), axis=1, keepdims=True)

    load_tokens.wait()
    order = lax.broadcasted_iota(jnp.int32, (slot_count, slot_count), 0)
    later = lax.broadcasted_iota(jnp.int32, (slot_count, slot_count), 1)
    before = jnp.where(order < later, 1.0, 0.0).astype(bf16)
    chosen = tokens[...]
    for place in range(groups):
        inside = (chosen >= place * group_rows) & (chosen < (place + 1) * group_rows)
        taken = jnp.where(inside, 1.0, 0.0)
        rank = jnp.dot(taken.astype(bf16), before, preferred_element_type=f32)
        ranks[place] = jnp.where(inside, rank, -1.0)
    kept = lax.broadcasted_iota(jnp.int32, (keep, slot_count), 0).astype(f32)
    mine = ranks[group]
    local = (chosen - group * group_rows + 1).astype(f32)
    for expert in range(chosen.shape[0]):
        hit = mine[expert : expert + 1, :] == kept
        slot_col[expert * keep : (expert + 1) * keep, :] = jnp.sum(
            jnp.where(hit, local[expert : expert + 1, :], 0.0), axis=1, keepdims=True
        )
    slots[...] = (
        jnp.sum(jnp.where(eye(slot_total), slot_col[...], 0.0), axis=0, keepdims=True) - 1.0
    )

    load_gain.wait()
    load_raw.wait()
    for unit in range(units):
        cols = pl.ds(unit * width, width)
        blocks[me, unit] = (raw[:, cols].astype(f32) * gain[:, cols]).astype(bf16)

    pl.semaphore_wait(barrier, len(peers))

    x0, y4 = own_x(0), own_y(half_units)
    x1, y5 = own_x(1), own_y(half_units + 1)
    part = blocks.at[me]
    pair_own = send(part, part, pair_send.at[3 * units], pair_recv.at[3 * units], partner)

    load_gates.wait()
    load_inputs.wait()
    contract = (((1,), (1,)), ((), ()))
    firsts = []
    for expert in range(local_experts):
        for copy in load_experts[expert]:
            copy.wait()
        gate_part = lax.dot_general(
            inputs[expert], gate_w[expert], contract, preferred_element_type=f32
        )
        up_part = lax.dot_general(
            inputs[expert], up_w[expert], contract, preferred_element_type=f32
        )
        hidden = (gate_part / (1.0 + jnp.exp(-gate_part)) * up_part).astype(bf16)
        scale_by = column(gates[expert : expert + 1, :])
        lines = pl.ds(expert * slot_count, slot_count)
        for place in range(2 * chips):
            value = jnp.dot(
                hidden,
                down_w[expert, :, place * width : (place + 1) * width],
                preferred_element_type=f32,
            )
            partial[place, lines, :] = (value * scale_by).astype(bf16)
        firsts.append(
            send(
                partial.at[pl.ds((1 - core) * chips, chips), lines],
                half_in.at[:, lines],
                first_send.at[expert],
                first_recv.at[expert],
                partner,
            )
        )

    for expert, copy in enumerate(firsts):
        copy.wait_recv()
        lines = pl.ds(expert * slot_count, slot_count)
        for chip in range(chips):
            chips_sum[chip, lines, :] = (
                partial[core * chips + chip, lines, :].astype(f32)
                + half_in[chip, lines, :].astype(f32)
            ).astype(bf16)
    reduces = [
        send(
            chips_sum.at[device // 2],
            chips_in.at[index],
            reduce_send.at[index],
            reduce_recv.at[index],
            device,
        )
        for index, device in enumerate((across, along_x, along_y))
    ]
    x2, y6 = own_x(2), own_y(half_units + 2)
    x3, y7 = own_x(3), own_y(half_units + 3)

    def accumulate(chip, unit):
        lines = pl.ds(pl.multiple_of(unit * width, width), width)
        left = blocks[pl.ds(2 * chip, 2), unit].reshape(pair, width)
        for index in range(col_tiles):
            cols = pl.ds(index * tile, tile)
            acc[chip, :, cols] += jnp.dot(left, weight[lines, cols], preferred_element_type=f32)

    def clear(chip, carry):
        acc[chip] = jnp.zeros(acc.shape[1:], f32)
        return carry

    lax.fori_loop(0, chips, clear, 0)
    row_acc[...] = jnp.zeros(row_acc.shape, f32)

    chip_own, chip_x, chip_y, chip_a = me // 2, along_x // 2, along_y // 2, across // 2

    def each(start, size, body):
        def step(index, carry):
            body(index)
            return carry

        lax.fori_loop(start, start + size, step, 0)

    def own(index):
        accumulate(chip_own, index)
        accumulate(chip_own, index + half_units)

    def near(index):
        accumulate(chip_x, index)
        accumulate(chip_y, index + half_units)

    def late(index):
        accumulate(chip_x, index + half_units)
        accumulate(chip_y, index)

    def far(index):
        accumulate(chip_a, index)
        accumulate(chip_a, index + half_units)

    pair_own.wait_recv()
    load_weight.wait()
    each(0, half_units, own)

    x0.wait_recv()
    px0 = to_partner(0, 0)
    y4.wait_recv()
    py4 = to_partner(1, half_units)
    a0, a4 = relay(0), relay(half_units)
    x1.wait_recv()
    px1 = to_partner(0, 1)
    y5.wait_recv()
    py5 = to_partner(1, half_units + 1)
    a1, a5 = relay(1), relay(half_units + 1)

    for copy in reduces:
        copy.wait_recv()
    total = chips_sum[me // 2].astype(f32)
    for index in range(3):
        total = total + chips_in[index].astype(f32)
    total = total.astype(bf16)
    for place in range(groups):
        for expert in range(local_experts):
            rank = ranks[place, pl.ds(group * local_experts + expert, 1), :]
            table = jnp.where(rank == kept, 1.0, 0.0).astype(bf16)
            outgoing[place, expert * keep : (expert + 1) * keep, :] = jnp.dot(
                table,
                total[expert * slot_count : (expert + 1) * slot_count],
                preferred_element_type=f32,
            ).astype(bf16)
    exchanges = []
    for d in range(1, groups):
        copy = pltpu.make_async_remote_copy(
            src_ref=outgoing.at[(group + d) % groups],
            dst_ref=rows.at[me, group],
            send_sem=group_send.at[d - 1],
            recv_sem=group_recv.at[d - 1],
            device_id=((group + d) % groups, me),
            device_id_type=MESH,
        )
        copy.start()
        exchanges.append(copy)
    rows[me, group] = outgoing[group]

    for copy in (px0, py4, px1, py5):
        copy.wait_recv()
    each(0, 2, near)
    x2.wait_recv()
    px2 = to_partner(0, 2)
    y6.wait_recv()
    py6 = to_partner(1, half_units + 2)

    for copy in exchanges:
        copy.wait_recv()
    groups_half = groups // 2
    rest = groups - groups_half
    row_x, row_y = rows_to(0, me, 0, groups, along_x), rows_to(1, me, 0, groups, along_y)
    row_own = rows_to(4, me, 0, groups, partner)

    x3.wait_recv()
    px3 = to_partner(0, 3)
    y7.wait_recv()
    py7 = to_partner(1, half_units + 3)
    for copy in (px2, py6, px3, py7):
        copy.wait_recv()
    each(2, 2, near)
    a0.wait_recv()
    pa0 = to_partner(2, 0)
    a4.wait_recv()
    pa4 = to_partner(2, half_units)

    row_x.wait_recv()
    row_ox = rows_to(2, along_x, 0, groups_half, along_y)
    row_px = rows_to(5, along_x, 0, groups, partner)
    row_y.wait_recv()
    row_oy = rows_to(3, along_y, groups_half, rest, along_x)
    row_py = rows_to(6, along_y, 0, groups, partner)
    a2, a6 = relay(2), relay(half_units + 2)
    a3, a7 = relay(3), relay(half_units + 3)
    last = [(own_x(half_units + step), own_y(step)) for step in range(half_units - 2)]

    a1.wait_recv()
    pa1 = to_partner(2, 1)
    a5.wait_recv()
    pa5 = to_partner(2, half_units + 1)
    for copy in (pa0, pa4, pa1, pa5):
        copy.wait_recv()
    each(0, 2, far)

    row_ox.wait_recv()
    row_oy.wait_recv()
    row_pa = rows_to(7, across, 0, groups, partner)
    for copy in (row_own, row_px, row_py, row_pa):
        copy.wait_recv()

    def placement(begin, size):
        line = lax.broadcasted_iota(jnp.int32, (size, slot_total), 0) + begin
        return jnp.where(slots[...] == line.astype(f32), 1.0, 0.0).astype(bf16)

    own_place = placement(me * tok_rows, tok_rows)

    def combine(source, squares):
        start = ((source % 2) * chips + source // 2) * width
        cols = pl.ds(pl.multiple_of(start, width), width)
        values = rows[source].reshape(slot_total, width)
        combined = raw[:, cols].astype(f32) + jnp.dot(
            own_place, values, preferred_element_type=f32
        )
        stream_ref[:, cols] = combined.astype(bf16)
        for piece in range(0, width, 128):
            value = combined[:, piece : piece + 128]
            squares = squares + value * value
        return squares

    squares = lax.fori_loop(0, members, combine, jnp.zeros((tok_rows, 128), f32))
    scale = lax.rsqrt(jnp.sum(squares, axis=1, keepdims=True) / feature_width + 1e-06)
    scale_row = jnp.sum(jnp.where(eye(tok_rows), scale, 0.0), axis=0, keepdims=True)
    scales[me] = jnp.broadcast_to(scale_row, scales.shape[1:])
    part = scales.at[me]
    scalings = [
        send(
            part, part, scale_send.at[d - 1], scale_recv.at[d - 1], lax.rem(me + d, members)
        )
        for d in range(1, members)
    ]
    last += [
        (own_x(half_units + step), own_y(step)) for step in range(half_units - 2, half_units)
    ]

    a2.wait_recv()
    pa2 = to_partner(2, 2)
    a6.wait_recv()
    pa6 = to_partner(2, half_units + 2)

    def multiply_rows(source):
        start = ((source % 2) * chips + source // 2) * width
        lines = pl.ds(pl.multiple_of(start, width), width)
        values = rows[source].reshape(slot_total, width).astype(f32)
        values = (values * gain[:, lines]).astype(bf16)
        for index in range(col_tiles):
            cols = pl.ds(index * tile, tile)
            row_acc[:, cols] += jnp.dot(values, weight[lines, cols], preferred_element_type=f32)

    each(0, members, multiply_rows)
    row_out[...] = row_acc[...].astype(bf16)

    def place_rows(chip):
        spread = placement(chip * pair, pair)
        for index in range(col_tiles):
            cols = pl.ds(index * tile, tile)
            acc[chip, :, cols] += jnp.dot(spread, row_out[:, cols], preferred_element_type=f32)

    each(0, chips, place_rows)

    a3.wait_recv()
    pa3 = to_partner(2, 3)
    a7.wait_recv()
    pa7 = to_partner(2, half_units + 3)
    for copy in (pa2, pa6, pa3, pa7):
        copy.wait_recv()
    each(2, 2, far)

    def finish(chip):
        def body(side, carry):
            scale_by = column(scales[2 * chip + side, 0:1, :])
            lines = pl.ds(pl.multiple_of(side * tok_rows, tok_rows), tok_rows)
            begin = pl.multiple_of(chip * pair + side * tok_rows, tok_rows)
            projected_ref[pl.ds(begin, tok_rows), :] = (acc[chip, lines, :] * scale_by).astype(
                bf16
            )
            return carry

        lax.fori_loop(0, 2, body, 0)

    drain = len(sent) - 2 * half_units
    passed = []
    for step, (near_x, near_y) in enumerate(last):
        near_x.wait_recv()
        px = to_partner(0, half_units + step)
        near_y.wait_recv()
        py = to_partner(1, step)
        passed.append((px, py))
        if step:
            for copy in passed[step - 1]:
                copy.wait_recv()
            each(step - 1, 1, late)
        if step == half_units - 2:
            for copy in scalings:
                copy.wait_recv()
            finish(chip_own)
            finish(chip_a)
            for copy in sent[:drain] + exchanges:
                copy.wait_send()
    for copy in passed[-1]:
        copy.wait_recv()
    each(half_units - 1, 1, late)
    finish(chip_x)
    finish(chip_y)

    for copy in sent[drain:]:
        copy.wait_send()


def communicate(
    groups, members, keep, inputs, gates, tokens, w_gate, w_up, w_down, residual, gain, w_qkv
):
    local_experts, slot_count, feature_width = inputs.shape
    tok_rows = residual.shape[0]
    row_total = local_experts * slot_count
    width = feature_width // members
    chips = members // 2
    columns = w_qkv.shape[1]
    slot_total = tokens.shape[0] * keep
    bf16, f32 = jnp.bfloat16, jnp.float32
    hbm = pl.BlockSpec(memory_space=pltpu.HBM)
    vmem = pl.BlockSpec(memory_space=pltpu.VMEM)
    dma = pltpu.SemaphoreType.DMA
    gate_t, up_t = jnp.swapaxes(w_gate, 1, 2), jnp.swapaxes(w_up, 1, 2)
    return pl.pallas_call(
        functools.partial(comm_kernel, groups, keep),
        in_specs=[hbm] * 9,
        out_specs=[vmem, vmem],
        out_shape=[
            pltpu.VMEM((tok_rows, feature_width), bf16),
            pltpu.VMEM((members * tok_rows, columns), bf16),
        ],
        scratch_shapes=[
            pltpu.VMEM(inputs.shape, bf16),
            pltpu.VMEM(gates.shape, f32),
            pltpu.VMEM(tokens.shape, jnp.int32),
            pltpu.VMEM(gain.shape, f32),
            pltpu.VMEM(gate_t.shape, bf16),
            pltpu.VMEM(up_t.shape, bf16),
            pltpu.VMEM(w_down.shape, bf16),
            pltpu.VMEM(residual.shape, bf16),
            pltpu.VMEM(w_qkv.shape, bf16),
            pltpu.VMEM((members, members, tok_rows, width), bf16),
            pltpu.VMEM((members, groups, local_experts * keep, width), bf16),
            pltpu.VMEM((chips, 2 * tok_rows, columns), f32),
            pltpu.VMEM((slot_total, columns), f32),
            pltpu.VMEM((slot_total, columns), bf16),
            pltpu.VMEM((groups,) + tokens.shape, f32),
            pltpu.VMEM((slot_total, 1), f32),
            pltpu.VMEM((1, slot_total), f32),
            pltpu.VMEM((members, 8, tok_rows), f32),
            pltpu.VMEM((members, row_total, width), bf16),
            pltpu.VMEM((chips, row_total, width), bf16),
            pltpu.VMEM((chips, row_total, width), bf16),
            pltpu.VMEM((chips - 1, row_total, width), bf16),
            pltpu.VMEM((groups, local_experts * keep, width), bf16),
            dma((6,)),
            dma((3 * local_experts,)),
            dma((local_experts,)),
            dma((local_experts,)),
            dma((3,)),
            dma((3,)),
            dma((groups - 1,)),
            dma((groups - 1,)),
            dma((3 * members,)),
            dma((3 * members,)),
            dma((3 * members + 1,)),
            dma((3 * members + 1,)),
            dma((8,)),
            dma((8,)),
            dma((members - 1,)),
            dma((members - 1,)),
        ],
        compiler_params=pltpu.CompilerParams(
            collective_id=0, has_side_effects=True, vmem_limit_bytes=58 * 1024 * 1024
        ),
    )(inputs, gates, tokens, gain, gate_t, up_t, w_down, residual, w_qkv)


def out_kernel(stream_ref, projected_ref, stream_hbm, projected_hbm, sem):
    copies = [
        pltpu.make_async_copy(projected_ref, projected_hbm, sem.at[0]),
        pltpu.make_async_copy(stream_ref, stream_hbm, sem.at[1]),
    ]
    for copy in copies:
        copy.start()
    for copy in copies:
        copy.wait()


def put_out(stream, projected):
    return pl.pallas_call(
        out_kernel,
        in_specs=[pl.BlockSpec(memory_space=pltpu.VMEM)] * 2,
        out_specs=[pl.BlockSpec(memory_space=pltpu.HBM)] * 2,
        out_shape=[jax.ShapeDtypeStruct(v.shape, v.dtype) for v in (stream, projected)],
        scratch_shapes=[pltpu.SemaphoreType.DMA((2,))],
        compiler_params=pltpu.CompilerParams(vmem_limit_bytes=8 * 1024 * 1024),
    )(stream, projected)


def plain_rows(
    expert_inputs, gates, w_gate, w_up, w_down, send_table, expert_count, tensor_count
):
    local_experts, slot_count, feature_width = expert_inputs.shape
    gate_part = jnp.einsum(
        "ecd,edf->ecf", expert_inputs, w_gate, preferred_element_type=jnp.float32
    )
    up_part = jnp.einsum("ecd,edf->ecf", expert_inputs, w_up, preferred_element_type=jnp.float32)
    hidden = (jax.nn.silu(gate_part) * up_part).astype(jnp.bfloat16)
    partial_value = (
        jnp.einsum("ecf,efd->ecd", hidden, w_down, preferred_element_type=jnp.float32)
        * gates[:, :, None]
    ).astype(jnp.bfloat16)
    row_total = local_experts * slot_count
    arrived = lax.all_to_all(
        partial_value.reshape(row_total, feature_width),
        "tensor",
        split_axis=1,
        concat_axis=0,
        tiled=True,
    ).reshape(tensor_count, local_experts, slot_count, -1)
    summed = jnp.sum(arrived.astype(jnp.float32), axis=0).astype(jnp.bfloat16)

    outgoing = jnp.einsum("zlkmj,mjf->zlkf", send_table, summed)
    incoming = lax.all_to_all(
        outgoing.reshape(expert_count, -1, outgoing.shape[-1]),
        "expert",
        split_axis=0,
        concat_axis=0,
        tiled=True,
    )
    incoming = incoming.reshape(-1, outgoing.shape[-1])
    return lax.all_gather(incoming, "tensor", axis=0, tiled=False)


def per_device(
    expert_inputs, gates, chosen_tokens, w_gate, w_up, w_down, residual, norm_gain, w_qkv
):
    expert_count = lax.axis_size("expert")
    tensor_count = lax.axis_size("tensor")
    my_group = lax.axis_index("expert")
    local_experts, slot_count, feature_width = expert_inputs.shape
    tok_rows = residual.shape[0]
    group_rows = tok_rows * tensor_count
    keep = min(slot_count, MOST * tensor_count)
    if tensor_count == 8:
        return put_out(
            *communicate(
                expert_count,
                tensor_count,
                keep,
                expert_inputs,
                gates,
                chosen_tokens,
                w_gate,
                w_up,
                w_down,
                residual,
                norm_gain[None, :],
                w_qkv,
            )
        )

    dest = chosen_tokens // group_rows
    earlier = jnp.arange(slot_count)[None, :] < jnp.arange(slot_count)[:, None]
    rank = jnp.sum(
        ((dest[:, :, None] == dest[:, None, :]) & earlier[None]).astype(jnp.int32), axis=2
    )
    kept = jnp.arange(keep, dtype=jnp.int32)
    mine = jnp.where(dest == my_group, rank, -1)
    token_at = jnp.sum(
        jnp.where(
            mine[:, None, :] == kept[None, :, None],
            (chosen_tokens % group_rows)[:, None, :] + 1,
            0,
        ),
        axis=2,
    ).reshape(1, -1) - 1

    local_dest = lax.dynamic_slice_in_dim(dest, my_group * local_experts, local_experts, 0)
    local_rank = lax.dynamic_slice_in_dim(rank, my_group * local_experts, local_experts, 0)
    send_table = (
        (local_dest[None, :, None, :] == jnp.arange(expert_count)[:, None, None, None])
        & (local_rank[None, :, None, :] == kept[None, None, :, None])
    ).astype(jnp.bfloat16)
    same = jnp.eye(local_experts, dtype=jnp.bfloat16)
    send_table = send_table[:, :, :, None, :] * same[None, :, None, :, None]
    residual_all = lax.all_gather(residual, "tensor", axis=0, tiled=True)
    rows = plain_rows(
        expert_inputs, gates, w_gate, w_up, w_down, send_table, expert_count, tensor_count
    )
    order = tuple(range(tensor_count))
    return finish(
        lax.axis_index("tensor").reshape(1),
        token_at,
        residual_all,
        rows,
        order,
        norm_gain[None, :],
        w_qkv,
        tok_rows,
    )


def solution(mesh):
    return jax.shard_map(
        per_device,
        mesh=mesh,
        in_specs=(
            P("expert", None, None),
            P("expert", None),
            P(),
            P("expert", None, "tensor"),
            P("expert", None, "tensor"),
            P("expert", "tensor", None),
            P(("expert", "tensor"), None),
            P(),
            P(None, "tensor"),
        ),
        out_specs=(P(("expert", "tensor"), None), P("expert", "tensor")),
        check_vma=False,
    )
```

time: 82.1 us -> 64.6 us (0.79)
  local copies, waits for them, and re-layouts: 8.48 us -> 0 us
  Pallas kernels: 70 us -> 63.7 us
  other arithmetic: 2.62 us -> 0 us
    pallas_call x1 -> x2, Pallas kernels: 70 us -> 63.7 us  [the longest x1 61.7 us: communicate(): pl.pallas_call(functools.partial(comm_kernel, groups, keep), in_specs=[hb...]
    unnamed x2 -> x0, local copies, waits for them, and re-layouts: 6.04 us -> none
    broadcast_in_dim x1 -> x0, local copies, waits for them, and re-layouts: 1.41 us -> none  [communicate(): gates[:, :, None]]
    select_n x2 -> x0, other arithmetic: 1.4 us -> none  [the longest x1 0.7 us: per_device(): mine = jnp.where(dest == my_group, rank, -1)]
where the time goes in v1:
time: 64.6 us; the launch traced here: 64.4 us
  Pallas kernels  63.7 us (99%)
    pallas_call x1, Pallas kernels, communicate(): pl.pallas_call(functools.partial(comm_kernel, groups, keep), in_specs=[hb...  61.7 us
    pallas_call x1, Pallas kernels, put_out(): pl.pallas_call(out_kernel, in_specs=[pl.BlockSpec(memory_space=pltpu.VMEM...  2.02 us

profile of v1, /device:TPU:0, one launch (start us, length us, event | category | flops | bytes accessed | tf_op | source)
XLA Modules:
  0.0 64.4 jit_solution(16104892689281951888)
XLA Ops:
  0.6 61.7 %shard_map.104 = (bf16[128,4096]{1,0:T(8,128)(2,1)S(1)}, bf16[1024,1536]{1,0:T(8,128)(2,1)S(1)}) custom-call(bf16[2,64,4096]{2,1,0:T(8,128)(2,1)} %inputs_hbm.1, f32[2,64]{1,0:T(2,128)} %gates_hbm.1, s32[8,64]{1,0:T(8,128)} %tokens_hbm.1, f32[1,4096]{1,0:T(1,128)} %bitcast.5, bf16[2,224,4096]{2,1,0:T(8,128)(2,1)} %bitcast.3, bf16[2,224,4096]{2,1,0:T(8,128)(2,1)} %bitcast.4, ...), custom_call_target="tpu_custom_call" | custom-call | tf_op jit(solution)/shard_map/pallas_call | solution.py:602
  62.4 2.0 %shard_map.105 = (bf16[128,4096]{1,0:T(8,128)(2,1)}, bf16[1024,1536]{1,0:T(8,128)(2,1)}) custom-call(bf16[128,4096]{1,0:T(8,128)(2,1)S(1)} %get-tuple-element.4.stream_ref, bf16[1024,1536]{1,0:T(8,128)(2,1)S(1)} %get-tuple-element.5.projected_ref), custom_call_target="tpu_custom_call" | custom-call | tf_op jit(solution)/shard_map/pallas_call | solution.py:669

commit v2 on v1

--- a/solution.py
+++ b/solution.py
@@ -143,6 +143,9 @@
     chips_sum,
     chips_in,
     outgoing,
+    squares,
+    own_place,
+    scale_cols,
     load_sem,
     expert_sem,
     first_send,
@@ -188,16 +191,16 @@
     load_gain = load(gain_hbm, gain, load_sem.at[2])
     load_raw = load(residual_hbm, raw, load_sem.at[3])
     load_inputs = load(inputs_hbm, inputs, load_sem.at[4])
-    load_experts = [
-        [
+
+    def load_expert(expert):
+        return [
             load(hbm.at[expert], vmem.at[expert], expert_sem.at[3 * expert + index])
             for index, (hbm, vmem) in enumerate(
                 ((gate_hbm, gate_w), (up_hbm, up_w), (down_hbm, down_w))
             )
         ]
-        for expert in range(local_experts)
-    ]
-    load_weight = load(weight_hbm, weight, load_sem.at[5])
+
+    load_experts = [load_expert(0)]
 
     barrier = pltpu.get_barrier_semaphore()
     peers = [(group, lax.rem(me + d, members)) for d in range(1, members)]
@@ -205,7 +208,8 @@
     for device in peers:
         pl.semaphore_signal(barrier, inc=1, device_id=device, device_id_type=MESH)
 
-    sent = []
+    def settle(ref, sem):
+        pltpu.make_async_copy(ref, ref, sem).wait()
 
     def send(source, target, send_sem, recv_sem, device):
         copy = pltpu.make_async_remote_copy(
@@ -217,32 +221,44 @@
             device_id_type=MESH,
         )
         copy.start()
-        sent.append(copy)
         return copy
 
-    def on_link(index, origin, unit, device):
+    half_rows = tok_rows // 2
+
+    def on_link(kind, index, origin, unit, device):
         part = blocks.at[origin, unit]
-        return send(part, part, link_send.at[index], link_recv.at[index], device)
-
-    def own_x(unit):
-        return on_link(unit, me, unit, along_x)
-
-    def own_y(unit):
-        return on_link(units + unit, me, unit, along_y)
-
-    def relay(unit):
-        if unit < half_units:
-            return on_link(2 * units + unit, along_x, unit, along_y)
-        return on_link(2 * units + unit, along_y, unit, along_x)
-
-    def to_partner(role, unit):
-        part = blocks.at[(along_x, along_y, across)[role], unit]
-        index = role * units + unit
-        return send(part, part, pair_send.at[index], pair_recv.at[index], partner)
+        send(part, part, link_send.at[kind], link_recv.at[index], device)
+
+    def own_pair(index, unit_x, unit_y):
+        on_link(0, index, me, unit_x, along_x)
+        on_link(1, index, me, unit_y, along_y)
+
+    def relay_pair(step):
+        on_link(2, units + step, along_x, step, along_y)
+        on_link(2, units + step, along_y, half_units + step, along_x)
+
+    def own_ends():
+        for side in range(2):
+            for kind, unit, device in ((0, units - 1, along_x), (1, half_units - 1, along_y)):
+                part = blocks.at[me, unit, pl.ds(side * half_rows, half_rows)]
+                send(
+                    part,
+                    part,
+                    link_send.at[kind],
+                    link_recv.at[units + half_units + side],
+                    device,
+                )
+
+    def to_partner(index, role, unit, start=0, size=tok_rows):
+        part = blocks.at[(along_x, along_y, across)[role], unit, pl.ds(start, size)]
+        send(part, part, pair_send.at[role], pair_recv.at[index], partner)
+
+    two_units = blocks.at[me, pl.ds(0, 2)]
+    one_unit = blocks.at[me, 0]
 
     def rows_to(index, origin, start, size, device):
         part = rows.at[origin, pl.ds(start, size)]
-        return send(part, part, row_send.at[index], row_recv.at[index], device)
+        return send(part, part, row_send, row_recv.at[index], device)
 
     def eye(size):
         shape = (size, size)
@@ -277,16 +293,18 @@
 
     load_gain.wait()
     load_raw.wait()
+    load_experts += [load_expert(expert) for expert in range(1, local_experts)]
     for unit in range(units):
         cols = pl.ds(unit * width, width)
         blocks[me, unit] = (raw[:, cols].astype(f32) * gain[:, cols]).astype(bf16)
 
     pl.semaphore_wait(barrier, len(peers))
 
-    x0, y4 = own_x(0), own_y(half_units)
-    x1, y5 = own_x(1), own_y(half_units + 1)
+    own_pair(0, 0, half_units)
+    own_pair(1, 1, half_units + 1)
+    own_pair(2, 2, half_units + 2)
     part = blocks.at[me]
-    pair_own = send(part, part, pair_send.at[3 * units], pair_recv.at[3 * units], partner)
+    send(part, part, pair_send.at[3], pair_recv.at[units + half_units + 2], partner)
 
     load_gates.wait()
     load_inputs.wait()
@@ -295,6 +313,8 @@
     for expert in range(local_experts):
         for copy in load_experts[expert]:
             copy.wait()
+        if expert == 0:
+            load_weight = load(weight_hbm, weight, load_sem.at[5])
         gate_part = lax.dot_general(
             inputs[expert], gate_w[expert], contract, preferred_element_type=f32
         )
@@ -315,7 +335,7 @@
             send(
                 partial.at[pl.ds((1 - core) * chips, chips), lines],
                 half_in.at[:, lines],
-                first_send.at[expert],
+                first_send,
                 first_recv.at[expert],
                 partner,
             )
@@ -329,25 +349,19 @@
                 partial[core * chips + chip, lines, :].astype(f32)
                 + half_in[chip, lines, :].astype(f32)
             ).astype(bf16)
-    reduces = [
-        send(
-            chips_sum.at[device // 2],
-            chips_in.at[index],
-            reduce_send.at[index],
-            reduce_recv.at[index],
-            device,
-        )
-        for index, device in enumerate((across, along_x, along_y))
-    ]
-    x2, y6 = own_x(2), own_y(half_units + 2)
-    x3, y7 = own_x(3), own_y(half_units + 3)
-
-    def accumulate(chip, unit):
+    for index, device in enumerate((across, along_x, along_y)):
+        send(chips_sum.at[device // 2], chips_in.at[index], reduce_send, reduce_recv, device)
+    own_pair(3, 3, half_units + 3)
+
+    def product(chip, unit, index):
         lines = pl.ds(pl.multiple_of(unit * width, width), width)
         left = blocks[pl.ds(2 * chip, 2), unit].reshape(pair, width)
+        cols = pl.ds(index * tile, tile)
+        return jnp.dot(left, weight[lines, cols], preferred_element_type=f32)
+
+    def accumulate(chip, unit):
         for index in range(col_tiles):
-            cols = pl.ds(index * tile, tile)
-            acc[chip, :, cols] += jnp.dot(left, weight[lines, cols], preferred_element_type=f32)
+            acc[chip, :, pl.ds(index * tile, tile)] += product(chip, unit, index)
 
     def clear(chip, carry):
         acc[chip] = jnp.zeros(acc.shape[1:], f32)
@@ -355,6 +369,7 @@
 
     lax.fori_loop(0, chips, clear, 0)
     row_acc[...] = jnp.zeros(row_acc.shape, f32)
+    squares[...] = jnp.zeros(squares.shape, f32)
 
     chip_own, chip_x, chip_y, chip_a = me // 2, along_x // 2, along_y // 2, across // 2
 
@@ -381,23 +396,36 @@
         accumulate(chip_a, index)
         accumulate(chip_a, index + half_units)
 
-    pair_own.wait_recv()
+    def forward(step):
+        settle(two_units, link_recv.at[step])
+        to_partner(step, 0, step)
+        to_partner(step, 1, half_units + step)
+
+    def forward_late(step):
+        settle(two_units, link_recv.at[half_units + step])
+        to_partner(half_units + step, 0, half_units + step)
+        to_partner(half_units + step, 1, step)
+
+    def forward_far(step):
+        settle(two_units, link_recv.at[units + step])
+        to_partner(units + step, 2, step)
+        to_partner(units + step, 2, half_units + step)
+
+    def arrive(kind, step):
+        settle(two_units, pair_recv.at[{"near": 0, "late": half_units, "far": units}[kind] + step])
+
+    forward(0)
+    forward(1)
+    relay_pair(0)
+    relay_pair(1)
+    settle(blocks.at[me], pair_recv.at[units + half_units + 2])
     load_weight.wait()
     each(0, half_units, own)
-
-    x0.wait_recv()
-    px0 = to_partner(0, 0)
-    y4.wait_recv()
-    py4 = to_partner(1, half_units)
-    a0, a4 = relay(0), relay(half_units)
-    x1.wait_recv()
-    px1 = to_partner(0, 1)
-    y5.wait_recv()
-    py5 = to_partner(1, half_units + 1)
-    a1, a5 = relay(1), relay(half_units + 1)
-
-    for copy in reduces:
-        copy.wait_recv()
+    arrive("near", 0)
+    arrive("near", 1)
+    each(0, 2, near)
+
+    settle(chips_in, reduce_recv)
     total = chips_sum[me // 2].astype(f32)
     for index in range(3):
         total = total + chips_in[index].astype(f32)
@@ -411,46 +439,65 @@
                 total[expert * slot_count : (expert + 1) * slot_count],
                 preferred_element_type=f32,
             ).astype(bf16)
-    exchanges = []
     for d in range(1, groups):
-        copy = pltpu.make_async_remote_copy(
+        pltpu.make_async_remote_copy(
             src_ref=outgoing.at[(group + d) % groups],
             dst_ref=rows.at[me, group],
-            send_sem=group_send.at[d - 1],
-            recv_sem=group_recv.at[d - 1],
+            send_sem=group_send,
+            recv_sem=group_recv,
             device_id=((group + d) % groups, me),
             device_id_type=MESH,
-        )
-        copy.start()
-        exchanges.append(copy)
+        ).start()
     rows[me, group] = outgoing[group]
 
-    for copy in (px0, py4, px1, py5):
-        copy.wait_recv()
-    each(0, 2, near)
-    x2.wait_recv()
-    px2 = to_partner(0, 2)
-    y6.wait_recv()
-    py6 = to_partner(1, half_units + 2)
-
-    for copy in exchanges:
-        copy.wait_recv()
+    forward(2)
+    arrive("near", 2)
+    each(2, 1, near)
+    forward(3)
+    arrive("near", 3)
+    each(3, 1, near)
+
+    settle(outgoing.at[pl.ds(0, groups - 1)], group_recv)
     groups_half = groups // 2
     rest = groups - groups_half
     row_x, row_y = rows_to(0, me, 0, groups, along_x), rows_to(1, me, 0, groups, along_y)
     row_own = rows_to(4, me, 0, groups, partner)
-
-    x3.wait_recv()
-    px3 = to_partner(0, 3)
-    y7.wait_recv()
-    py7 = to_partner(1, half_units + 3)
-    for copy in (px2, py6, px3, py7):
-        copy.wait_recv()
-    each(2, 2, near)
-    a0.wait_recv()
-    pa0 = to_partner(2, 0)
-    a4.wait_recv()
-    pa4 = to_partner(2, half_units)
+    relay_pair(2)
+    forward_far(0)
+    forward_far(1)
+
+    def placement(begin, size):
+        line = lax.broadcasted_iota(jnp.int32, (size, slot_total), 0) + begin
+        return jnp.where(slots[...] == line.astype(f32), 1.0, 0.0).astype(bf16)
+
+    own_place[...] = placement(me * tok_rows, tok_rows)
+
+    def take_rows(source):
+        start = ((source % 2) * chips + source // 2) * width
+        part = pl.ds(pl.multiple_of(start, width), width)
+        values = rows[source].reshape(slot_total, width)
+        combined = raw[:, part].astype(f32) + jnp.dot(
+            own_place[...], values, preferred_element_type=f32
+        )
+        stream_ref[:, part] = combined.astype(bf16)
+        total = squares[...]
+        for piece in range(0, width, 128):
+            value = combined[:, piece : piece + 128]
+            total = total + value * value
+        squares[...] = total
+        values = (values.astype(f32) * gain[:, part]).astype(bf16)
+        for index in range(col_tiles):
+            cols = pl.ds(index * tile, tile)
+            row_acc[:, cols] += jnp.dot(values, weight[part, cols], preferred_element_type=f32)
+
+    def take_pair(chip):
+        each(2 * chip, 2, take_rows)
+
+    row_own.wait_recv()
+    take_pair(chip_own)
+    arrive("far", 0)
+    arrive("far", 1)
+    each(0, 2, far)
 
     row_x.wait_recv()
     row_ox = rows_to(2, along_x, 0, groups_half, along_y)
@@ -458,73 +505,31 @@
     row_y.wait_recv()
     row_oy = rows_to(3, along_y, groups_half, rest, along_x)
     row_py = rows_to(6, along_y, 0, groups, partner)
-    a2, a6 = relay(2), relay(half_units + 2)
-    a3, a7 = relay(3), relay(half_units + 3)
-    last = [(own_x(half_units + step), own_y(step)) for step in range(half_units - 2)]
-
-    a1.wait_recv()
-    pa1 = to_partner(2, 1)
-    a5.wait_recv()
-    pa5 = to_partner(2, half_units + 1)
-    for copy in (pa0, pa4, pa1, pa5):
-        copy.wait_recv()
-    each(0, 2, far)
-
+    relay_pair(3)
+    own_pair(half_units, half_units, 0)
+    row_px.wait_recv()
+    take_pair(chip_x)
+    row_py.wait_recv()
+    take_pair(chip_y)
+    forward_far(2)
     row_ox.wait_recv()
     row_oy.wait_recv()
     row_pa = rows_to(7, across, 0, groups, partner)
-    for copy in (row_own, row_px, row_py, row_pa):
-        copy.wait_recv()
-
-    def placement(begin, size):
-        line = lax.broadcasted_iota(jnp.int32, (size, slot_total), 0) + begin
-        return jnp.where(slots[...] == line.astype(f32), 1.0, 0.0).astype(bf16)
-
-    own_place = placement(me * tok_rows, tok_rows)
-
-    def combine(source, squares):
-        start = ((source % 2) * chips + source // 2) * width
-        cols = pl.ds(pl.multiple_of(start, width), width)
-        values = rows[source].reshape(slot_total, width)
-        combined = raw[:, cols].astype(f32) + jnp.dot(
-            own_place, values, preferred_element_type=f32
-        )
-        stream_ref[:, cols] = combined.astype(bf16)
-        for piece in range(0, width, 128):
-            value = combined[:, piece : piece + 128]
-            squares = squares + value * value
-        return squares
-
-    squares = lax.fori_loop(0, members, combine, jnp.zeros((tok_rows, 128), f32))
-    scale = lax.rsqrt(jnp.sum(squares, axis=1, keepdims=True) / feature_width + 1e-06)
+    own_pair(half_units + 1, half_units + 1, 1)
+    arrive("far", 2)
+    each(2, 1, far)
+    row_pa.wait_recv()
+    take_pair(chip_a)
+
+    scale = lax.rsqrt(jnp.sum(squares[...], axis=1, keepdims=True) / feature_width + 1e-06)
     scale_row = jnp.sum(jnp.where(eye(tok_rows), scale, 0.0), axis=0, keepdims=True)
     scales[me] = jnp.broadcast_to(scale_row, scales.shape[1:])
     part = scales.at[me]
-    scalings = [
-        send(
-            part, part, scale_send.at[d - 1], scale_recv.at[d - 1], lax.rem(me + d, members)
-        )
-        for d in range(1, members)
-    ]
-    last += [
-        (own_x(half_units + step), own_y(step)) for step in range(half_units - 2, half_units)
-    ]
-
-    a2.wait_recv()
-    pa2 = to_partner(2, 2)
-    a6.wait_recv()
-    pa6 = to_partner(2, half_units + 2)
-
-    def multiply_rows(source):
-        start = ((source % 2) * chips + source // 2) * width
-        lines = pl.ds(pl.multiple_of(start, width), width)
-        values = rows[source].reshape(slot_total, width).astype(f32)
-        values = (values * gain[:, lines]).astype(bf16)
-        for index in range(col_tiles):
-            cols = pl.ds(index * tile, tile)
-            row_acc[:, cols] += jnp.dot(values, weight[lines, cols], preferred_element_type=f32)
-
-    each(0, members, multiply_rows)
+    for d in range(1, members):
+        send(part, part, scale_send, scale_recv, lax.rem(me + d, members))
+    own_pair(half_units + 2, half_units + 2, 2)
+    own_ends()
+
     row_out[...] = row_acc[...].astype(bf16)
 
     def place_rows(chip):
@@ -533,55 +538,78 @@
             cols = pl.ds(index * tile, tile)
             acc[chip, :, cols] += jnp.dot(spread, row_out[:, cols], preferred_element_type=f32)
 
+    forward_far(3)
     each(0, chips, place_rows)
-
-    a3.wait_recv()
-    pa3 = to_partner(2, 3)
-    a7.wait_recv()
-    pa7 = to_partner(2, half_units + 3)
-    for copy in (pa2, pa6, pa3, pa7):
-        copy.wait_recv()
-    each(2, 2, far)
+    arrive("far", 3)
+    each(3, 1, far)
+    forward_late(0)
+    arrive("late", 0)
+    each(0, 1, late)
+    forward_late(1)
+    arrive("late", 1)
+    each(1, 1, late)
 
     def finish(chip):
         def body(side, carry):
-            scale_by = column(scales[2 * chip + side, 0:1, :])
             lines = pl.ds(pl.multiple_of(side * tok_rows, tok_rows), tok_rows)
-            begin = pl.multiple_of(chip * pair + side * tok_rows, tok_rows)
-            projected_ref[pl.ds(begin, tok_rows), :] = (acc[chip, lines, :] * scale_by).astype(
-                bf16
-            )
+            begin = pl.multiple_of((2 * chip + side) * tok_rows, tok_rows)
+            projected_ref[pl.ds(begin, tok_rows), :] = (
+                acc[chip, lines, :] * scale_cols[2 * chip + side]
+            ).astype(bf16)
             return carry
 
         lax.fori_loop(0, 2, body, 0)
 
-    drain = len(sent) - 2 * half_units
-    passed = []
-    for step, (near_x, near_y) in enumerate(last):
-        near_x.wait_recv()
-        px = to_partner(0, half_units + step)
-        near_y.wait_recv()
-        py = to_partner(1, step)
-        passed.append((px, py))
-        if step:
-            for copy in passed[step - 1]:
-                copy.wait_recv()
-            each(step - 1, 1, late)
-        if step == half_units - 2:
-            for copy in scalings:
-                copy.wait_recv()
-            finish(chip_own)
-            finish(chip_a)
-            for copy in sent[:drain] + exchanges:
-                copy.wait_send()
-    for copy in passed[-1]:
-        copy.wait_recv()
-    each(half_units - 1, 1, late)
-    finish(chip_x)
-    finish(chip_y)
-
-    for copy in sent[drain:]:
-        copy.wait_send()
+    def close(chip, unit, start):
+        first = pl.multiple_of(2 * chip * tok_rows + start, half_rows)
+        left = blocks[pl.ds(2 * chip, 2), unit, pl.ds(start, half_rows), :].reshape(
+            tok_rows, width
+        )
+        lines = pl.ds(unit * width, width)
+        for index in range(col_tiles):
+            cols = pl.ds(index * tile, tile)
+            value = jnp.dot(left, weight[lines, cols], preferred_element_type=f32)
+            for side in range(2):
+                rows_in = pl.ds(side * tok_rows + start, half_rows)
+                piece = value[side * half_rows : (side + 1) * half_rows]
+                piece = (acc[chip, rows_in, cols] + piece) * scale_cols[
+                    2 * chip + side, pl.ds(start, half_rows), :
+                ]
+                projected_ref[pl.ds(first + side * tok_rows, half_rows), cols] = piece.astype(
+                    bf16
+                )
+
+    forward_late(2)
+    settle(scales.at[pl.ds(0, members - 1)], scale_recv)
+
+    def turn(source):
+        scale_cols[source] = column(scales[source, 0:1, :])
+
+    each(0, members, turn)
+    finish(chip_own)
+    finish(chip_a)
+    arrive("late", 2)
+    each(2, 1, late)
+    settle(half_in, first_send)
+    settle(chips_in, reduce_send)
+    settle(outgoing.at[pl.ds(0, groups - 1)], group_send)
+    settle(rows.at[pl.ds(0, 7)], row_send)
+    settle(scales.at[pl.ds(0, members - 1)], scale_send)
+    settle(blocks.at[me], link_send.at[2])
+    for role in (2, 3):
+        settle(blocks.at[me], pair_send.at[role])
+
+    for side in range(2):
+        settle(one_unit, link_recv.at[units + half_units + side])
+        for role, unit in enumerate((units - 1, half_units - 1)):
+            to_partner(units + half_units + side, role, unit, side * half_rows, half_rows)
+    for side in range(2):
+        settle(one_unit, pair_recv.at[units + half_units + side])
+        close(chip_x, units - 1, side * half_rows)
+        close(chip_y, half_units - 1, side * half_rows)
+    for role in range(2):
+        settle(blocks.at[me], link_send.at[role])
+        settle(blocks.at[me], pair_send.at[role])
 
 
 def communicate(
@@ -592,6 +620,7 @@
     row_total = local_experts * slot_count
     width = feature_width // members
     chips = members // 2
+    units = members
     columns = w_qkv.shape[1]
     slot_total = tokens.shape[0] * keep
     bf16, f32 = jnp.bfloat16, jnp.float32
@@ -631,22 +660,25 @@
             pltpu.VMEM((chips, row_total, width), bf16),
             pltpu.VMEM((chips - 1, row_total, width), bf16),
             pltpu.VMEM((groups, local_experts * keep, width), bf16),
+            pltpu.VMEM((tok_rows, 128), f32),
+            pltpu.VMEM((tok_rows, slot_total), bf16),
+            pltpu.VMEM((members, tok_rows, 1), f32),
             dma((6,)),
             dma((3 * local_experts,)),
+            dma,
             dma((local_experts,)),
-            dma((local_experts,)),
+            dma,
+            dma,
+            dma,
+            dma,
             dma((3,)),
-            dma((3,)),
-            dma((groups - 1,)),
-            dma((groups - 1,)),
-            dma((3 * members,)),
-            dma((3 * members,)),
-            dma((3 * members + 1,)),
-            dma((3 * members + 1,)),
+            dma((units + units // 2 + 2,)),
+            dma((4,)),
+            dma((units + units // 2 + 3,)),
+            dma,
             dma((8,)),
-            dma((8,)),
-            dma((members - 1,)),
-            dma((members - 1,)),
+            dma,
+            dma,
         ],
         compiler_params=pltpu.CompilerParams(
             collective_id=0, has_side_effects=True, vmem_limit_bytes=58 * 1024 * 1024

time: 64.6 us -> 61.9 us (0.958)
  Pallas kernels: 63.7 us -> 60.9 us
    pallas_call x1, Pallas kernels: 61.7 us -> 58.9 us  [communicate(): pl.pallas_call(functools.partial(comm_kernel, groups, keep), in_specs=[hb...]
where the time goes in v2:
time: 61.9 us; the launch traced here: 61.7 us
  Pallas kernels  60.9 us (98%)
  between operations  0.8 us (1%)
    pallas_call x1, Pallas kernels, communicate(): pl.pallas_call(functools.partial(comm_kernel, groups, keep), in_specs=[hb...  58.9 us
    pallas_call x1, Pallas kernels, put_out(): pl.pallas_call(out_kernel, in_specs=[pl.BlockSpec(memory_space=pltpu.VMEM...  2.02 us

profile of v2, /device:TPU:0, one launch (start us, length us, event | category | flops | bytes accessed | tf_op | source)
XLA Modules:
  0.0 61.7 jit_solution(10893090879865446751)
XLA Ops:
  0.6 58.9 %shard_map.104 = (bf16[128,4096]{1,0:T(8,128)(2,1)S(1)}, bf16[1024,1536]{1,0:T(8,128)(2,1)S(1)}) custom-call(bf16[2,64,4096]{2,1,0:T(8,128)(2,1)} %inputs_hbm.1, f32[2,64]{1,0:T(2,128)} %gates_hbm.1, s32[8,64]{1,0:T(8,128)} %tokens_hbm.1, f32[1,4096]{1,0:T(1,128)} %bitcast.5, bf16[2,224,4096]{2,1,0:T(8,128)(2,1)} %bitcast.3, bf16[2,224,4096]{2,1,0:T(8,128)(2,1)} %bitcast.4, ...), custom_call_target="tpu_custom_call" | custom-call | tf_op jit(solution)/shard_map/pallas_call | solution.py:631
  59.5 2.0 %shard_map.105 = (bf16[128,4096]{1,0:T(8,128)(2,1)}, bf16[1024,1536]{1,0:T(8,128)(2,1)}) custom-call(bf16[128,4096]{1,0:T(8,128)(2,1)S(1)} %get-tuple-element.4.stream_ref, bf16[1024,1536]{1,0:T(8,128)(2,1)S(1)} %get-tuple-element.5.projected_ref), custom_call_target="tpu_custom_call" | custom-call | tf_op jit(solution)/shard_map/pallas_call | solution.py:701
